TPU v7x, 32 devices: a whole 2x2x4 slice. The times are simulated.
32 devices in a mesh: dp: 4 (over x, core), seq: 8 (over z, y).
Axes of the slice: x: 2, y: 2, z: 4, core: 2. Of those that a mesh axis runs over, the one named last changes fastest.
Arguments:
- block_input: bfloat16 [16384, 2560], P(('dp', 'seq')), may hold values from -6 to 6
- w_query: bfloat16 [2560, 2560], P('dp', 'seq'), may hold values from -4 to 4
- w_keyval: bfloat16 [2560, 512], P('dp', 'seq'), may hold values from -0.125 to 0.125
- w_out: bfloat16 [2560, 2560], P('dp', 'seq'), may hold values from -2 to 2
- gain_attn: bfloat16 [2560], P(('dp', 'seq')), may hold values from 0.5 to 1.5
- w_gate: bfloat16 [2560, 7680], P('dp', 'seq'), may hold values from -0.125 to 0.125
- w_up: bfloat16 [2560, 7680], P('dp', 'seq'), may hold values from -0.125 to 0.125
- w_down: bfloat16 [2560, 7680], P('dp', 'seq'), may hold values from -0.0625 to 0.0625
- gain_mlp: bfloat16 [2560], P(('dp', 'seq')), may hold values from 0.5 to 1.5
- cotangent: bfloat16 [16384, 2560], P(('dp', 'seq')), may hold values from -6 to 6
Outputs:
- output_rows: bfloat16 [16384, 2560], P(('dp', 'seq'))
- grad_input: float32 [16384, 2560], P(('dp', 'seq'))
- grad_w_query: float32 [2560, 2560], P('dp', 'seq')
- grad_w_keyval: float32 [2560, 512], P('dp', 'seq')
- grad_w_out: float32 [2560, 2560], P('dp', 'seq')
- grad_gain_attn: float32 [2560], P(('dp', 'seq'))
- grad_w_gate: float32 [2560, 7680], P('dp', 'seq')
- grad_w_up: float32 [2560, 7680], P('dp', 'seq')
- grad_w_down: float32 [2560, 7680], P('dp', 'seq')
- grad_gain_mlp: float32 [2560], P(('dp', 'seq'))
All inputs are finite; a program needn't handle non-finite values.
Results may differ from a plain program's by a relative error of at most 0.019.
The roundings to bfloat16 on the way count: a program that leaves them out, or rounds other values in their place, can miss the bound.
Values may be sent and summed in bfloat16 or wider, within the bound.
A program may use at most 576 MiB of HBM per device.

v0:
```python
import jax
import jax.numpy as jnp
from jax import lax
from jax.sharding import PartitionSpec as P

HEADS = 10
HD = 256
WINDOW = 2048


def shifted(shard, axis, by):
    length = lax.axis_size(axis)
    pairs = [(i, i + by) for i in range(length) if 0 <= i + by < length]
    return lax.ppermute(shard, axis, pairs)


def norm_rows(values, gain):
    return values * lax.rsqrt(jnp.mean(values * values, axis=-1, keepdims=True) + 1e-06) * gain


def rotate(values, positions):
    rope_width = values.shape[-1] // 2
    half_width = rope_width // 2
    frequency = 10000.0 ** (-jnp.arange(half_width, dtype=jnp.float32) / half_width)
    angles = positions.astype(jnp.float32)[:, None] * frequency[None, :]
    cosine = jnp.cos(angles)
    sine_part = jnp.sin(angles)
    first_half = values[..., :half_width]
    second_half = values[..., half_width:rope_width]
    unturned = values[..., rope_width:]
    return jnp.concatenate(
        [
            first_half * cosine - second_half * sine_part,
            second_half * cosine + first_half * sine_part,
            unturned,
        ],
        axis=-1,
    )


def gelu_tanh(v):
    return jax.nn.gelu(v, approximate=True)


def contract_rows(left, right):
    return lax.dot_general(
        left, right, (((0,), (0,)), ((), ())), preferred_element_type=jnp.float32
    )


def contract_last(left, right):
    return lax.dot_general(
        left, right, (((1,), (1,)), ((), ())), preferred_element_type=jnp.float32
    )


def local(
    block_input, w_query, w_keyval, w_out, gain_attn, w_gate, w_up, w_down, gain_mlp, cotangent
):
    row_count = block_input.shape[0]
    seq_size = lax.axis_size("seq")
    seq_place = lax.axis_index("seq")
    depth = min((WINDOW + row_count - 2) // row_count, seq_size - 1)
    score_scale = HD ** (-0.5)
    positions = seq_place * row_count + jnp.arange(row_count, dtype=jnp.int32)
    column_part = (
        lax.all_gather(w_query, "seq", axis=1, tiled=True),
        lax.all_gather(w_keyval, "seq", axis=1, tiled=True),
        lax.all_gather(w_out, "seq", axis=1, tiled=True),
        lax.all_gather(w_gate, "seq", axis=1, tiled=True),
        lax.all_gather(w_up, "seq", axis=1, tiled=True),
        lax.all_gather(w_down, "seq", axis=1, tiled=True),
        lax.all_gather(gain_attn, "seq", axis=0, tiled=True),
        lax.all_gather(gain_mlp, "seq", axis=0, tiled=True),
    )
    query_full, keyval_full, out_full, gate_full, up_full, down_full, gain_one, gain_two = (
        lax.all_gather(column_part[0], "dp", axis=0, tiled=True),
        lax.all_gather(column_part[1], "dp", axis=0, tiled=True),
        lax.all_gather(column_part[2], "dp", axis=0, tiled=True),
        lax.all_gather(column_part[3], "dp", axis=0, tiled=True),
        lax.all_gather(column_part[4], "dp", axis=0, tiled=True),
        lax.all_gather(column_part[5], "dp", axis=0, tiled=True),
        lax.all_gather(column_part[6], "dp", axis=0, tiled=True),
        lax.all_gather(column_part[7], "dp", axis=0, tiled=True),
    )
    inputs = block_input.astype(jnp.float32)
    normed_one_f, norm_one_pull = jax.vjp(norm_rows, inputs, gain_one.astype(jnp.float32))
    normed_one = normed_one_f.astype(jnp.bfloat16)
    query_raw = jnp.dot(normed_one, query_full, preferred_element_type=jnp.float32)
    keyval_raw = jnp.dot(normed_one, keyval_full, preferred_element_type=jnp.float32)

    def turn_rows(v):
        return rotate(v, positions)

    query_rot, query_pull = jax.vjp(
        turn_rows, query_raw.reshape(row_count, HEADS, HD).transpose(1, 0, 2)
    )
    key_rot, key_pull = jax.vjp(turn_rows, keyval_raw[:, :HD])
    queries = query_rot.astype(jnp.bfloat16).reshape(HEADS * row_count, HD)
    keyval_own = jnp.concatenate([key_rot, keyval_raw[:, HD:]], axis=1).astype(jnp.bfloat16)

    def pass_forward(carried, unused):
        moved = shifted(carried, "seq", 1)
        return (moved, moved)

    _, earlier = lax.scan(pass_forward, keyval_own, None, length=depth)
    keyval_all = jnp.concatenate([keyval_own[None], earlier], axis=0).reshape(
        (depth + 1) * row_count, 2 * HD
    )
    key_rows = keyval_all[:, :HD]
    value_rows = keyval_all[:, HD:]
    offsets = jnp.arange(depth + 1, dtype=jnp.int32)
    key_pos = (
        (seq_place - offsets)[:, None] * row_count + jnp.arange(row_count, dtype=jnp.int32)[None, :]
    ).reshape(-1)
    query_pos = jnp.tile(positions, HEADS)
    distance = query_pos[:, None] - key_pos[None, :]
    allowed = (distance >= 0) & (distance < WINDOW) & (key_pos[None, :] >= 0)

    def score_block():
        raw_scores = contract_last(queries, key_rows) * score_scale
        return jnp.where(allowed, raw_scores, -1e30)

    scores = score_block()
    row_max = jnp.max(scores, axis=1, keepdims=True)
    exponent = jnp.exp(scores - row_max)
    row_total = jnp.sum(exponent, axis=1, keepdims=True)
    probs = exponent / row_total
    log_total = row_max + jnp.log(row_total)
    mixed_heads = jnp.dot(
        probs.astype(jnp.bfloat16), value_rows, preferred_element_type=jnp.float32
    )
    mixed_low = (
        mixed_heads.reshape(HEADS, row_count, HD)
        .transpose(1, 0, 2)
        .reshape(row_count, HEADS * HD)
        .astype(jnp.bfloat16)
    )
    resid = inputs + contract_last(mixed_low, out_full)
    normed_two_f, norm_two_pull = jax.vjp(norm_rows, resid, gain_two.astype(jnp.float32))
    normed_two = normed_two_f.astype(jnp.bfloat16)
    gate_pre = jnp.dot(normed_two, gate_full, preferred_element_type=jnp.float32)
    upward = jnp.dot(normed_two, up_full, preferred_element_type=jnp.float32)
    gelu_value, gelu_pull = jax.vjp(gelu_tanh, gate_pre)
    hidden = (gelu_value * upward).astype(jnp.bfloat16)
    output_rows = (resid + contract_last(hidden, down_full)).astype(jnp.bfloat16)
    back_part = (
        lax.all_gather(w_query, "seq", axis=1, tiled=True),
        lax.all_gather(w_keyval, "seq", axis=1, tiled=True),
        lax.all_gather(w_out, "seq", axis=1, tiled=True),
        lax.all_gather(w_gate, "seq", axis=1, tiled=True),
        lax.all_gather(w_up, "seq", axis=1, tiled=True),
        lax.all_gather(w_down, "seq", axis=1, tiled=True),
    )
    query_back, keyval_back, out_back, gate_back, up_back, down_back = (
        lax.all_gather(back_part[0], "dp", axis=0, tiled=True),
        lax.all_gather(back_part[1], "dp", axis=0, tiled=True),
        lax.all_gather(back_part[2], "dp", axis=0, tiled=True),
        lax.all_gather(back_part[3], "dp", axis=0, tiled=True),
        lax.all_gather(back_part[4], "dp", axis=0, tiled=True),
        lax.all_gather(back_part[5], "dp", axis=0, tiled=True),
    )
    upstream = cotangent.astype(jnp.float32)
    grad_hidden = jnp.dot(cotangent, down_back, preferred_element_type=jnp.float32)
    grad_gate = gelu_pull(grad_hidden * upward)[0].astype(jnp.bfloat16)
    grad_upward = (grad_hidden * gelu_value).astype(jnp.bfloat16)
    grad_normed_two = contract_last(grad_gate, gate_back) + contract_last(grad_upward, up_back)
    grad_resid_part, grad_gain_two = norm_two_pull(grad_normed_two)
    grad_resid = upstream + grad_resid_part
    normed_two_seq, cotangent_seq = (
        lax.all_gather(normed_two, "seq", axis=0, tiled=True),
        lax.all_gather(cotangent, "seq", axis=0, tiled=True),
    )
    gate_cols, upward_cols, hidden_cols = (
        lax.all_to_all(grad_gate, "seq", split_axis=1, concat_axis=0, tiled=True),
        lax.all_to_all(grad_upward, "seq", split_axis=1, concat_axis=0, tiled=True),
        lax.all_to_all(hidden, "seq", split_axis=1, concat_axis=0, tiled=True),
    )
    left_rows = normed_two_seq
    mlp_share = lax.psum_scatter(
        jnp.concatenate(
            [
                contract_rows(left_rows, gate_cols),
                contract_rows(left_rows, upward_cols),
                contract_rows(cotangent_seq, hidden_cols),
            ],
            axis=1,
        ).astype(jnp.bfloat16),
        "dp",
        scatter_dimension=0,
        tiled=True,
    ).astype(jnp.float32)
    attn_low = grad_resid.astype(jnp.bfloat16)
    grad_mixed = jnp.dot(attn_low, out_back, preferred_element_type=jnp.float32).astype(
        jnp.bfloat16
    )
    grad_heads = (
        grad_mixed.reshape(row_count, HEADS, HD).transpose(1, 0, 2).reshape(HEADS * row_count, HD)
    )
    probs_again = jnp.exp(score_block() - log_total)
    grad_probs = contract_last(grad_heads, value_rows)
    grad_scores = (
        probs_again * (grad_probs - jnp.sum(probs_again * grad_probs, axis=1, keepdims=True))
    ).astype(jnp.bfloat16)
    grad_queries = jnp.dot(grad_scores, key_rows, preferred_element_type=jnp.float32) * score_scale
    grad_keys_all = contract_rows(grad_scores, queries) * score_scale
    grad_values_all = contract_rows(probs_again.astype(jnp.bfloat16), grad_heads)
    grad_keyval_all = jnp.concatenate([grad_keys_all, grad_values_all], axis=1).reshape(
        depth + 1, row_count, 2 * HD
    )

    def pass_backward(carried, piece_grad):
        return (
            shifted((carried + piece_grad).astype(jnp.bfloat16), "seq", -1).astype(jnp.float32),
            None,
        )

    returned, _ = lax.scan(
        pass_backward, jnp.zeros((row_count, 2 * HD), jnp.float32), grad_keyval_all[1:][::-1]
    )
    grad_keyval = grad_keyval_all[0] + returned
    grad_keys_raw = key_pull(grad_keyval[:, :HD])[0]
    grad_keyval_raw = jnp.concatenate([grad_keys_raw, grad_keyval[:, HD:]], axis=1).astype(
        jnp.bfloat16
    )
    grad_query_raw = (
        query_pull(grad_queries.reshape(HEADS, row_count, HD))[0]
        .transpose(1, 0, 2)
        .reshape(row_count, HEADS * HD)
        .astype(jnp.bfloat16)
    )
    grad_normed_one = contract_last(grad_query_raw, query_back) + contract_last(
        grad_keyval_raw, keyval_back
    )
    grad_in_part, grad_gain_one = norm_one_pull(grad_normed_one)
    grad_input = grad_resid + grad_in_part
    normed_one_seq, attn_low_seq = (
        lax.all_gather(normed_one, "seq", axis=0, tiled=True),
        lax.all_gather(attn_low, "seq", axis=0, tiled=True),
    )
    query_cols, keyval_cols, mixed_cols = (
        lax.all_to_all(grad_query_raw, "seq", split_axis=1, concat_axis=0, tiled=True),
        lax.all_to_all(grad_keyval_raw, "seq", split_axis=1, concat_axis=0, tiled=True),
        lax.all_to_all(mixed_low, "seq", split_axis=1, concat_axis=0, tiled=True),
    )
    left_rows = normed_one_seq
    attn_share = lax.psum_scatter(
        jnp.concatenate(
            [
                contract_rows(left_rows, query_cols),
                contract_rows(left_rows, keyval_cols),
                contract_rows(attn_low_seq, mixed_cols),
            ],
            axis=1,
        ).astype(jnp.bfloat16),
        "dp",
        scatter_dimension=0,
        tiled=True,
    ).astype(jnp.float32)
    gain_shares = (
        lax.psum_scatter(grad_gain_one, ("dp", "seq"), scatter_dimension=0, tiled=True),
        lax.psum_scatter(grad_gain_two, ("dp", "seq"), scatter_dimension=0, tiled=True),
    )
    query_width = w_query.shape[1]
    keyval_width = w_keyval.shape[1]
    ff_width = w_gate.shape[1]
    grad_w_query = attn_share[:, :query_width]
    grad_w_keyval = attn_share[:, query_width : query_width + keyval_width]
    grad_w_out = attn_share[:, query_width + keyval_width :]
    return (
        output_rows,
        grad_input,
        grad_w_query,
        grad_w_keyval,
        grad_w_out,
        gain_shares[0],
        mlp_share[:, :ff_width],
        mlp_share[:, ff_width : 2 * ff_width],
        mlp_share[:, 2 * ff_width :],
        gain_shares[1],
    )


def solution(mesh):
    placed = (
        P(("dp", "seq"), None),
        P("dp", "seq"),
        P("dp", "seq"),
        P("dp", "seq"),
        P(("dp", "seq")),
        P("dp", "seq"),
        P("dp", "seq"),
        P("dp", "seq"),
        P(("dp", "seq")),
        P(("dp", "seq"), None),
    )
    return jax.shard_map(
        local,
        mesh=mesh,
        in_specs=placed,
        out_specs=(
            P(("dp", "seq"), None),
            P(("dp", "seq"), None),
            P("dp", "seq"),
            P("dp", "seq"),
            P("dp", "seq"),
            P(("dp", "seq")),
            P("dp", "seq"),
            P("dp", "seq"),
            P("dp", "seq"),
            P(("dp", "seq")),
        ),
        check_vma=False,
    )
```

profile of v0, /device:TPU:0, one launch (start us, length us, event | category | flops | bytes accessed | tf_op | source)
XLA Modules:
  0.0 3644.4 jit_solution(13936530598048494936)
XLA Ops:
  10.6 37.0 %all_gather.76 = bf16[640,512]{0,1:T(8,128)(2,1)} all-gather(bf16[640,64]{0,1:T(8,128)(2,1)} %param.16), channel_id=1, replica_groups=mesh['dp'=4,'seq'=8] {'seq'}, dimensions={1}, use_global_device_ids=true | all-gather | bytes 737280 | tf_op jit(solution)/shard_map/all_gather | solution.py:68
  47.6 30.3 all-gather.18.cloned.1.call-done
  78.0 62.6 %all-gather.24.cloned.1.call-done = bf16[640,2560]{0,1:T(8,128)(2,1)} async-done(((bf16[640,320]{0,1:T(8,128)(2,1)}), bf16[640,2560]{0,1:T(8,128)(2,1)}) %all-gather.24.cloned.1.call-update) | async-done | bytes 3276816 | tf_op jit(solution)/shard_map/all_gather | solution.py:69
  140.7 143.1 %all-gather.28.cloned.1.call-done = bf16[640,7680]{0,1:T(8,128)(2,1)} async-done(((bf16[640,960]{0,1:T(8,128)(2,1)}), bf16[640,7680]{0,1:T(8,128)(2,1)}) %all-gather.28.cloned.1.call-update) | async-done | bytes 9830416 | tf_op jit(solution)/shard_map/all_gather | solution.py:70
  283.8 142.4 %all-gather.32.cloned.1.call-done = bf16[640,7680]{0,1:T(8,128)(2,1)} async-done(((bf16[640,960]{0,1:T(8,128)(2,1)}), bf16[640,7680]{0,1:T(8,128)(2,1)}) %all-gather.32.cloned.1.call-update) | async-done | bytes 9830416 | tf_op jit(solution)/shard_map/all_gather | solution.py:71
  426.3 142.3 %all-gather.36.cloned.1.call-done = bf16[640,7680]{0,1:T(8,128)(2,1)} async-done(((bf16[640,960]{0,1:T(8,128)(2,1)}), bf16[640,7680]{0,1:T(8,128)(2,1)}) %all-gather.36.cloned.1.call-update) | async-done | bytes 9830416 | tf_op jit(solution)/shard_map/all_gather | solution.py:72
  610.0 61.6 %while.23 = (s32[]{:T(128)}, bf16[512,512]{1,0:T(8,128)(2,1)S(1)}, bf16[4,512,512]{2,1,0:T(8,128)(2,1)}, s32[]{:T(128)}) while((s32[]{:T(128)}, bf16[512,512]{1,0:T(8,128)(2,1)S(1)}, bf16[4,512,512]{2,1,0:T(8,128)(2,1)}, s32[]{:T(128)}) %tuple.62), condition=%wide.region_2.3_spmd, body=%wide.region_1.2_spmd.sunk | while | flops 2 | bytes 4194409 | solution.py:106
  704.0 29.9 fusion.58
  798.1 206.0 %all-gather.30.cloned.1.call-done = bf16[2560,7680]{0,1:T(8,128)(2,1)} async-done(((bf16[640,7680]{0,1:T(8,128)(2,1)}), bf16[2560,7680]{0,1:T(8,128)(2,1)}) %all-gather.30.cloned.1.call-update) | async-done | bytes 39321616 | tf_op jit(solution)/shard_map/all_gather | solution.py:80
  1004.1 32.0 fusion.61
  1036.1 204.9 %all-gather.34.cloned.1.call-done = bf16[2560,7680]{0,1:T(8,128)(2,1)} async-done(((bf16[640,7680]{0,1:T(8,128)(2,1)}), bf16[2560,7680]{0,1:T(8,128)(2,1)}) %all-gather.34.cloned.1.call-update) | async-done | bytes 39321616 | tf_op jit(solution)/shard_map/all_gather | solution.py:81
  1241.1 32.3 fusion.62
  1273.4 204.8 %all-gather.38.cloned.1.call-done = bf16[2560,7680]{0,1:T(8,128)(2,1)} async-done(((bf16[640,7680]{0,1:T(8,128)(2,1)}), bf16[2560,7680]{0,1:T(8,128)(2,1)}) %all-gather.38.cloned.1.call-update) | async-done | bytes 39321616 | tf_op jit(solution)/shard_map/all_gather | solution.py:82
  1478.2 39.7 %multiply_convert_fusion.1 = (bf16[512,7680]{1,0:T(8,128)(2,1)}, bf16[512,7680]{1,0:T(8,128)(2,1)}, bf16[512,7680]{1,0:T(8,128)(2,1)}) fusion(f32[512,7680]{1,0:T(8,128)} %fusion.61, f32[512,7680]{1,0:T(8,128)} %fusion.62, bf16[512,2560]{1,0:T(8,128)(2,1)S(1)} %copy-done.4, bf16[2560,7680]{0,1:T(8,128)(2,1)} %all-gather.38.cloned.1.call-done), kind=kOutput, calls=%fused_computation.27 | convolution fusion | flops 20234895360 | bytes 96993280 | tf_op jit(solution)/shard_map/dot_general | solution.py:164
  1573.6 196.7 %all-to-all-done.5 = bf16[512,8,960]{0,2,1:T(8,128)(2,1)} async-done(((bf16[512,8,960]{0,2,1:T(8,128)(2,1)}), bf16[512,8,960]{0,2,1:T(8,128)(2,1)}, u32[]{:S(2)}, u32[]{:S(2)}) %all-to-all-start.5) | async-done | bytes 7864352 | tf_op jit(solution)/shard_map/all_to_all | solution.py:177
  1770.3 60.0 %all-to-all-start.4 = ((bf16[512,8,960]{0,2,1:T(8,128)(2,1)}), bf16[512,8,960]{0,2,1:T(8,128)(2,1)}, u32[]{:S(2)}, u32[]{:S(2)}) async-start(bf16[512,8,960]{0,2,1:T(8,128)(2,1)} %bitcast.107), calls=%async_computation.4 | async-start | bytes 15728640 | tf_op jit(solution)/shard_map/all_to_all | solution.py:176
  1878.5 180.1 %all-to-all-done.4 = bf16[512,8,960]{0,2,1:T(8,128)(2,1)} async-done(((bf16[512,8,960]{0,2,1:T(8,128)(2,1)}), bf16[512,8,960]{0,2,1:T(8,128)(2,1)}, u32[]{:S(2)}, u32[]{:S(2)}) %all-to-all-start.4) | async-done | bytes 7864352 | tf_op jit(solution)/shard_map/all_to_all | solution.py:176
  2058.7 44.9 %all-to-all-start.3 = ((bf16[512,8,960]{0,2,1:T(8,128)(2,1)}), bf16[512,8,960]{0,2,1:T(8,128)(2,1)}, u32[]{:S(2)}, u32[]{:S(2)}) async-start(bf16[512,8,960]{0,2,1:T(8,128)(2,1)} %bitcast.108), calls=%async_computation.3 | async-start | bytes 15728640 | tf_op jit(solution)/shard_map/all_to_all | solution.py:175
  2137.3 202.1 %all-to-all-done.3 = bf16[512,8,960]{0,2,1:T(8,128)(2,1)} async-done(((bf16[512,8,960]{0,2,1:T(8,128)(2,1)}), bf16[512,8,960]{0,2,1:T(8,128)(2,1)}, u32[]{:S(2)}, u32[]{:S(2)}) %all-to-all-start.3) | async-done | bytes 7864352 | tf_op jit(solution)/shard_map/all_to_all | solution.py:175
  2339.4 57.7 %all-to-all-start.2 = ((bf16[512,8,320]{0,2,1:T(8,128)(2,1)}), bf16[512,8,320]{0,2,1:T(8,128)(2,1)}, u32[]{:S(2)}, u32[]{:S(2)}) async-start(bf16[512,8,320]{0,2,1:T(8,128)(2,1)} %bitcast.116), calls=%async_computation.2 | async-start | bytes 5242880 | tf_op jit(solution)/shard_map/all_to_all | solution.py:244
  2453.6 123.2 %all-gather.46.cloned.1.call-done = bf16[4096,2560]{1,0:T(8,128)(2,1)} async-done(((bf16[512,2560]{1,0:T(8,128)(2,1)}), bf16[4096,2560]{1,0:T(8,128)(2,1)}) %all-gather.46.cloned.1.call-update) | async-done | bytes 20971536 | tf_op jit(solution)/shard_map/all_gather | solution.py:172
  2665.0 33.6 multiply_reduce_fusion
  2698.6 41.6 %multiply_convert_fusion = bf16[5120,2560]{0,1:T(8,128)(2,1)} fusion(f32[5120,2560]{0,1:T(8,128)} %get-tuple-element.115, f32[5120,2560]{0,1:T(8,128)} %get-tuple-element.110, f32[5120]{0:T(1024)S(1)} %get-tuple-element.114, f32[5120]{0:T(1024)S(1)} %log_add_fusion), kind=kLoop, calls=%fused_computation.5 | loop fusion | flops 52428800 | bytes 131112960 | tf_op jit(solution)/shard_map/convert_element_type | solution.py:204
  2769.5 195.0 %while.24 = (s32[]{:T(128)}, f32[512,512]{1,0:T(8,128)S(1)}, f32[4,512,512]{2,1,0:T(8,128)}, s32[]{:T(128)}, s32[]{:T(128)}) while((s32[]{:T(128)}, f32[512,512]{1,0:T(8,128)S(1)}, f32[4,512,512]{2,1,0:T(8,128)}, s32[]{:T(128)}, s32[]{:T(128)}) %tuple.102), condition=%wide.region_9.10_spmd.clone, body=%wide.region_8.9_spmd.clone.sunk | while | flops 1048579 | bytes 6291571 | solution.py:218
  2772.3 70.2 %collective-permute-done.1 = bf16[512,512]{1,0:T(8,128)(2,1)S(1)} collective-permute-done((bf16[512,512]{1,0:T(8,128)(2,1)S(1)}, bf16[512,512]{1,0:T(8,128)(2,1)S(1)}, u32[]{:S(2)}, u32[]{:S(2)}) %collective-permute-start.1) | collective-permute-done | bytes 524320 | tf_op jit(solution)/shard_map/while/body/eval_jaxpr/ppermute | solution.py:14
  2845.5 40.5 %collective-permute-done.1 = bf16[512,512]{1,0:T(8,128)(2,1)S(1)} collective-permute-done((bf16[512,512]{1,0:T(8,128)(2,1)S(1)}, bf16[512,512]{1,0:T(8,128)(2,1)S(1)}, u32[]{:S(2)}, u32[]{:S(2)}) %collective-permute-start.1) | collective-permute-done | bytes 524320 | tf_op jit(solution)/shard_map/while/body/eval_jaxpr/ppermute | solution.py:14
  2888.9 34.0 collective-permute-done.1
  2925.8 38.5 %collective-permute-done.1 = bf16[512,512]{1,0:T(8,128)(2,1)S(1)} collective-permute-done((bf16[512,512]{1,0:T(8,128)(2,1)S(1)}, bf16[512,512]{1,0:T(8,128)(2,1)S(1)}, u32[]{:S(2)}, u32[]{:S(2)}) %collective-permute-start.1) | collective-permute-done | bytes 524320 | tf_op jit(solution)/shard_map/while/body/eval_jaxpr/ppermute | solution.py:14
  3068.4 30.6 all-to-all-done
  3112.0 352.8 %all-gather.42.cloned.1.call-done = bf16[4096,2560]{1,0:T(8,128)(2,1)} async-done(((bf16[512,2560]{1,0:T(8,128)(2,1)}), bf16[4096,2560]{1,0:T(8,128)(2,1)}) %all-gather.42.cloned.1.call-update) | async-done | bytes 20971536 | tf_op jit(solution)/shard_map/all_gather | solution.py:239
  3494.2 44.3 %all-reduce.10 = (f32[2560]{0:T(1024)S(1)}, f32[2560]{0:T(1024)S(1)}) all-reduce(f32[2560]{0:T(1024)S(1)} %get-tuple-element.69, f32[2560]{0:T(1024)S(1)} %copy-done.51), channel_id=3, replica_groups=mesh['dp'=4,'seq'=8] {'dp','seq'}, use_global_device_ids=true, to_apply=%region_13.14.clone | all-reduce | flops 5120 | bytes 40960
  3600.8 32.9 reduce-scatter.7.cloned.1.call-done
  (306 shorter events, 737.1 us)
Async XLA Ops:
  7.2 70.7 %all-gather.18.cloned.1.call-start = ((), (), s32[]{:S(2)}) async-start(), calls=%async_computation.8 | async-start | bytes 3686400 | tf_op jit(solution)/shard_map/all_gather | solution.py:67
  7.9 132.7 %all-gather.24.cloned.1.call-start = ((), (), s32[]{:S(2)}) async-start(), calls=%async_computation.11 | async-start | bytes 3686400 | tf_op jit(solution)/shard_map/all_gather | solution.py:69
  8.7 275.1 %all-gather.28.cloned.1.call-start = ((), (), s32[]{:S(2)}) async-start(), calls=%async_computation.13 | async-start | bytes 11059200 | tf_op jit(solution)/shard_map/all_gather | solution.py:70
  9.4 416.8 %all-gather.32.cloned.1.call-start = ((), (), s32[]{:S(2)}) async-start(), calls=%async_computation.15 | async-start | bytes 11059200 | tf_op jit(solution)/shard_map/all_gather | solution.py:71
  10.0 558.7 %all-gather.36.cloned.1.call-start = ((), (), s32[]{:S(2)}) async-start(), calls=%async_computation.17 | async-start | bytes 11059200 | tf_op jit(solution)/shard_map/all_gather | solution.py:72
  10.6 593.0 %all-gather.22.cloned.1.call-start = ((), (), s32[]{:S(2)}) async-start(), calls=%async_computation.10 | async-start | bytes 3276800 | tf_op jit(solution)/shard_map/all_gather | solution.py:78
  47.6 632.8 %all-gather.20.cloned.1.call-start = ((), (), s32[]{:S(2)}) async-start(), calls=%async_computation.9 | async-start | bytes 16384000 | tf_op jit(solution)/shard_map/all_gather | solution.py:77
  77.9 698.8 %all-gather.26.cloned.1.call-start = ((), (), s32[]{:S(2)}) async-start(), calls=%async_computation.12 | async-start | bytes 16384000 | tf_op jit(solution)/shard_map/all_gather | solution.py:79
  140.6 863.5 %all-gather.30.cloned.1.call-start = ((), (), s32[]{:S(2)}) async-start(), calls=%async_computation.14 | async-start | bytes 49152000 | tf_op jit(solution)/shard_map/all_gather | solution.py:80
  283.7 957.3 %all-gather.34.cloned.1.call-start = ((), (), s32[]{:S(2)}) async-start(), calls=%async_computation.16 | async-start | bytes 49152000 | tf_op jit(solution)/shard_map/all_gather | solution.py:81
  426.3 1051.9 %all-gather.38.cloned.1.call-start = ((), (), s32[]{:S(2)}) async-start(), calls=%async_computation.18 | async-start | bytes 49152000 | tf_op jit(solution)/shard_map/all_gather | solution.py:82
  568.7 1836.0 %all-gather.44.cloned.1.call-start = ((), (), s32[]{:S(2)}) async-start(), calls=%async_computation.21 | async-start | bytes 23592960 | tf_op jit(solution)/shard_map/all_gather | solution.py:171
  610.2 14.1 collective-permute-start
  625.2 15.4 collective-permute-start
  641.5 14.6 collective-permute-start
  656.9 13.9 collective-permute-start
  796.7 1780.0 %all-gather.46.cloned.1.call-start = ((), (), s32[]{:S(2)}) async-start(), calls=%async_computation.22 | async-start | bytes 23592960 | tf_op jit(solution)/shard_map/all_gather | solution.py:172
  797.5 2261.8 %all-gather.40.cloned.1.call-start = ((), (), s32[]{:S(2)}) async-start(), calls=%async_computation.19 | async-start | bytes 23592960 | tf_op jit(solution)/shard_map/all_gather | solution.py:238
  1036.1 442.1 %copy-start.4 = (bf16[512,2560]{1,0:T(8,128)(2,1)S(1)}, bf16[512,2560]{1,0:T(8,128)(2,1)}, u32[]{:S(2)}) copy-start(bf16[512,2560]{1,0:T(8,128)(2,1)} %param.23) | copy-start | bytes 7864324
  1528.5 241.8 %all-to-all-start.5 = ((bf16[512,8,960]{0,2,1:T(8,128)(2,1)}), bf16[512,8,960]{0,2,1:T(8,128)(2,1)}, u32[]{:S(2)}, u32[]{:S(2)}) async-start(bf16[512,8,960]{0,2,1:T(8,128)(2,1)} %bitcast.109), calls=%async_computation.5 | async-start | bytes 15728640 | tf_op jit(solution)/shard_map/all_to_all | solution.py:177
  1770.3 288.3 %all-to-all-start.4 = ((bf16[512,8,960]{0,2,1:T(8,128)(2,1)}), bf16[512,8,960]{0,2,1:T(8,128)(2,1)}, u32[]{:S(2)}, u32[]{:S(2)}) async-start(bf16[512,8,960]{0,2,1:T(8,128)(2,1)} %bitcast.107), calls=%async_computation.4 | async-start | bytes 15728640 | tf_op jit(solution)/shard_map/all_to_all | solution.py:176
  1830.4 1634.4 %all-gather.42.cloned.1.call-start = ((), (), s32[]{:S(2)}) async-start(), calls=%async_computation.20 | async-start | bytes 23592960 | tf_op jit(solution)/shard_map/all_gather | solution.py:239
  2058.7 280.7 %all-to-all-start.3 = ((bf16[512,8,960]{0,2,1:T(8,128)(2,1)}), bf16[512,8,960]{0,2,1:T(8,128)(2,1)}, u32[]{:S(2)}, u32[]{:S(2)}) async-start(bf16[512,8,960]{0,2,1:T(8,128)(2,1)} %bitcast.108), calls=%async_computation.3 | async-start | bytes 15728640 | tf_op jit(solution)/shard_map/all_to_all | solution.py:175
  2339.4 644.9 %all-to-all-start.2 = ((bf16[512,8,320]{0,2,1:T(8,128)(2,1)}), bf16[512,8,320]{0,2,1:T(8,128)(2,1)}, u32[]{:S(2)}, u32[]{:S(2)}) async-start(bf16[512,8,320]{0,2,1:T(8,128)(2,1)} %bitcast.116), calls=%async_computation.2 | async-start | bytes 5242880 | tf_op jit(solution)/shard_map/all_to_all | solution.py:244
  2397.1 1191.5 %reduce-scatter.9.cloned.1.call-start = ((), (), s32[]{:S(2)}) async-start(), calls=%async_computation.24 | async-start | bytes 18841600
  2771.0 71.5 %collective-permute-start.1 = (bf16[512,512]{1,0:T(8,128)(2,1)S(1)}, bf16[512,512]{1,0:T(8,128)(2,1)S(1)}, u32[]{:S(2)}, u32[]{:S(2)}) collective-permute-start(bf16[512,512]{1,0:T(8,128)(2,1)S(1)} %fusion.105), channel_id=1, source_target_pairs={{1,0},{2,1},{3,2},{4,3},{5,4},{6,5},{7,6},{9,8},{10,9},{11,10},{12... | collective-permute-start | bytes 1572872 | tf_op jit(solution)/shard_map/while/body/eval_jaxpr/ppermute | solution.py:14
  2844.2 41.8 %collective-permute-start.1 = (bf16[512,512]{1,0:T(8,128)(2,1)S(1)}, bf16[512,512]{1,0:T(8,128)(2,1)S(1)}, u32[]{:S(2)}, u32[]{:S(2)}) collective-permute-start(bf16[512,512]{1,0:T(8,128)(2,1)S(1)} %fusion.105), channel_id=1, source_target_pairs={{1,0},{2,1},{3,2},{4,3},{5,4},{6,5},{7,6},{9,8},{10,9},{11,10},{12... | collective-permute-start | bytes 1572872 | tf_op jit(solution)/shard_map/while/body/eval_jaxpr/ppermute | solution.py:14
  2887.6 35.3 collective-permute-start.1
  2924.5 39.8 %collective-permute-start.1 = (bf16[512,512]{1,0:T(8,128)(2,1)S(1)}, bf16[512,512]{1,0:T(8,128)(2,1)S(1)}, u32[]{:S(2)}, u32[]{:S(2)}) collective-permute-start(bf16[512,512]{1,0:T(8,128)(2,1)S(1)} %fusion.105), channel_id=1, source_target_pairs={{1,0},{2,1},{3,2},{4,3},{5,4},{6,5},{7,6},{9,8},{10,9},{11,10},{12... | collective-permute-start | bytes 1572872 | tf_op jit(solution)/shard_map/while/body/eval_jaxpr/ppermute | solution.py:14
  2984.3 21.7 all-to-all-start.1
  3006.0 93.0 %all-to-all-start = ((bf16[512,8,320]{0,2,1:T(8,128)(2,1)}), bf16[512,8,320]{0,2,1:T(8,128)(2,1)S(1)}, u32[]{:S(2)}, u32[]{:S(2)}) async-start(bf16[512,8,320]{0,2,1:T(8,128)(2,1)} %bitcast.119), calls=%async_computation | async-start | bytes 5242880 | tf_op jit(solution)/shard_map/all_to_all | solution.py:242
  3025.2 608.5 %reduce-scatter.7.cloned.1.call-start = ((), (), s32[]{:S(2)}) async-start(), calls=%async_computation.23 | async-start | bytes 4915200
  (61 other events, 2327.7 us)
Sparse Core Ops, SparseCore 0:
  10.2 67.6 all-gather.17
  80.1 60.4 all-gather.23
  142.8 140.8 all-gather.27
  285.8 140.3 all-gather.31
  428.2 140.3 all-gather.35
  570.1 23.6 all-gather.21
  595.4 84.9 all-gather.19
  682.0 84.9 all-gather.25
  768.5 235.5 all-gather.29
  1005.5 235.5 all-gather.33
  1242.6 235.5 all-gather.37
  1479.6 570.2 all-gather.43
  2051.4 525.3 all-gather.45
  2578.7 480.5 all-gather.39
  3060.7 404.0 all-gather.41
  3467.2 121.2 reduce-scatter.8
  3591.0 42.7 reduce-scatter.6
where the time goes:
time: 3650 us; the launch traced here: 3640 us
  waiting for transfers between devices  2520 us (69%)
  matrix products  491 us (13%)
  starting transfers between devices  213 us (6%)
  local copies, waits for them, and re-layouts  166 us (5%)
  other arithmetic  130 us (4%)
  blocking collectives  110 us (3%)
    all_gather x1, waiting for transfers between devices, local(): lax.all_gather(attn_low, 'seq', axis=0, tiled=True)  353 us
    ppermute x8, waiting for transfers between devices, shifted(): return lax.ppermute(shard, axis, pairs)  225 us
    all_gather x1, waiting for transfers between devices, local(): lax.all_gather(column_part[3], 'dp', axis=0, tiled=True)  206 us
    all_gather x1, waiting for transfers between devices, local(): lax.all_gather(column_part[4], 'dp', axis=0, tiled=True)  205 us
    all_gather x1, waiting for transfers between devices, local(): lax.all_gather(column_part[5], 'dp', axis=0, tiled=True)  205 us
    all_to_all x1, waiting for transfers between devices, local(): lax.all_to_all(grad_gate, 'seq', split_axis=1, concat_axis=0, tiled=True)  202 us
    all_to_all x1, waiting for transfers between devices, local(): lax.all_to_all(hidden, 'seq', split_axis=1, concat_axis=0, tiled=True)  197 us
    dot_general x8, matrix products, contract_last(): lax.dot_general(left, right, (((1,), (1,)), ((), ())), preferred_element_...  185 us
  transfers between devices with their start and end apart: 31, of which 26 were waited for; matrix products, arithmetic and copies ran while one was open for 21% of the time, Pallas kernels for 0%

commit v1 on v0

--- a/solution.py
+++ b/solution.py
@@ -6,6 +6,28 @@
 HEADS = 10
 HD = 256
 WINDOW = 2048
+
+
+def joined_along(parts, dim):
+    parts = jnp.moveaxis(parts, 0, dim)
+    dims = parts.shape
+    return parts.reshape(*dims[:dim], dims[dim] * dims[dim + 1], *dims[dim + 2 :])
+
+
+def collect(value, axis, dim):
+    size = lax.axis_size(axis)
+    pairs = [(i, (i + 1) % size) for i in range(size)]
+    back = [(b, a) for a, b in pairs]
+    lower, upper = ([], [])
+    for step in range(size - 1):
+        if step % 2 == 0:
+            lower.append(lax.ppermute(lower[-1] if lower else value, axis, pairs))
+        else:
+            upper.append(lax.ppermute(upper[-1] if upper else value, axis, back))
+    blocks = jnp.stack([*lower[::-1], value, *upper])
+    shift = lax.axis_index(axis) - len(lower)
+    blocks = blocks[(jnp.arange(size) - shift) % size]
+    return joined_along(blocks, dim)
 
 
 def shifted(shard, axis, by):
@@ -77,7 +99,7 @@
         lax.all_gather(column_part[0], "dp", axis=0, tiled=True),
         lax.all_gather(column_part[1], "dp", axis=0, tiled=True),
         lax.all_gather(column_part[2], "dp", axis=0, tiled=True),
-        lax.all_gather(column_part[3], "dp", axis=0, tiled=True),
+        collect(column_part[3], "dp", 0),
         lax.all_gather(column_part[4], "dp", axis=0, tiled=True),
         lax.all_gather(column_part[5], "dp", axis=0, tiled=True),
         lax.all_gather(column_part[6], "dp", axis=0, tiled=True),

time: 3650 us -> 3960 us (1.085)
  waiting for transfers between devices: 2520 us -> 2700 us
  local copies, waits for them, and re-layouts: 166 us -> 280 us
    ppermute x0 -> x3, waiting for transfers between devices: none -> 716 us  [the longest x2 716 us: collect(): lower.append(lax.ppermute(lower[-1] if lower else value, axis, pairs))]
    all_gather x1, waiting for transfers between devices: 206 us -> 0.01 us  [local(): lax.all_gather(back_part[3], 'dp', axis=0, tiled=True)]
    all_gather x1, waiting for transfers between devices: 205 us -> 0.01 us  [local(): lax.all_gather(column_part[4], 'dp', axis=0, tiled=True)]
    all_gather x1, waiting for transfers between devices: 205 us -> 0.01 us  [local(): lax.all_gather(column_part[5], 'dp', axis=0, tiled=True)]
    all_gather x1, waiting for transfers between devices: 123 us -> 193 us  [local(): lax.all_gather(cotangent, 'seq', axis=0, tiled=True)]
    gather x0 -> x6, local copies, waits for them, and re-layouts: none -> 67.8 us  [collect(): blocks = blocks[(jnp.arange(size) - shift) % size]]
    unnamed x140 -> x149, local copies, waits for them, and re-layouts: 57.5 us -> 89.9 us
  transfers between devices with their start and end apart: 31 -> 34, of which waited for: 26 -> 25; matrix products, arithmetic and copies ran while one was open for 21% -> 23% of each run, Pallas kernels for 0% -> 0%
where the time goes in v1:
time: 3960 us; the launch traced here: 3950 us
  waiting for transfers between devices  2700 us (68%)
  matrix products  484 us (12%)
  local copies, waits for them, and re-layouts  280 us (7%)
  starting transfers between devices  197 us (5%)
  other arithmetic  162 us (4%)
  blocking collectives  108 us (3%)
    ppermute x2, waiting for transfers between devices, collect(): lower.append(lax.ppermute(lower[-1] if lower else value, axis, pairs))  716 us
    all_gather x1, waiting for transfers between devices, local(): lax.all_gather(attn_low, 'seq', axis=0, tiled=True)  359 us
    ppermute x8, waiting for transfers between devices, shifted(): return lax.ppermute(shard, axis, pairs)  228 us
    all_to_all x1, waiting for transfers between devices, local(): lax.all_to_all(hidden, 'seq', split_axis=1, concat_axis=0, tiled=True)  216 us
    all_gather x1, waiting for transfers between devices, local(): lax.all_gather(cotangent, 'seq', axis=0, tiled=True)  193 us
    all_to_all x1, waiting for transfers between devices, local(): lax.all_to_all(grad_upward, 'seq', split_axis=1, concat_axis=0, tiled=True)  190 us
    dot_general x8, matrix products, contract_last(): lax.dot_general(left, right, (((1,), (1,)), ((), ())), preferred_element_...  184 us
    all_to_all x1, waiting for transfers between devices, local(): lax.all_to_all(grad_gate, 'seq', split_axis=1, concat_axis=0, tiled=True)  180 us
  transfers between devices with their start and end apart: 34, of which 25 were waited for; matrix products, arithmetic and copies ran while one was open for 23% of the time, Pallas kernels for 0%

profile of v1, /device:TPU:0, one launch (start us, length us, event | category | flops | bytes accessed | tf_op | source)
XLA Modules:
  0.0 3949.7 jit_solution(17756213686028022970)
XLA Ops:
  10.6 37.0 all_gather.75
  47.6 30.3 all-gather.18.cloned.1.call-done
  78.0 62.6 %all-gather.24.cloned.1.call-done = bf16[640,2560]{0,1:T(8,128)(2,1)} async-done(((bf16[640,320]{0,1:T(8,128)(2,1)}), bf16[640,2560]{0,1:T(8,128)(2,1)}) %all-gather.24.cloned.1.call-update) | async-done | bytes 3276816 | tf_op jit(solution)/shard_map/all_gather | solution.py:91
  140.7 143.1 %all-gather.30.cloned.1.call-done = bf16[640,7680]{0,1:T(8,128)(2,1)} async-done(((bf16[640,960]{0,1:T(8,128)(2,1)}), bf16[640,7680]{0,1:T(8,128)(2,1)}) %all-gather.30.cloned.1.call-update) | async-done | bytes 9830416 | tf_op jit(solution)/shard_map/all_gather | solution.py:93
  283.8 142.4 %all-gather.34.cloned.1.call-done = bf16[640,7680]{0,1:T(8,128)(2,1)} async-done(((bf16[640,960]{0,1:T(8,128)(2,1)}), bf16[640,7680]{0,1:T(8,128)(2,1)}) %all-gather.34.cloned.1.call-update) | async-done | bytes 9830416 | tf_op jit(solution)/shard_map/all_gather | solution.py:94
  426.3 142.3 %all-gather.28.cloned.1.call-done = bf16[640,7680]{0,1:T(8,128)(2,1)} async-done(((bf16[640,960]{0,1:T(8,128)(2,1)}), bf16[640,7680]{0,1:T(8,128)(2,1)}) %all-gather.28.cloned.1.call-update) | async-done | bytes 9830416 | tf_op jit(solution)/shard_map/all_gather | solution.py:92
  610.0 61.7 %while.23 = (s32[]{:T(128)}, bf16[512,512]{1,0:T(8,128)(2,1)S(1)}, bf16[4,512,512]{2,1,0:T(8,128)(2,1)}, s32[]{:T(128)}) while((s32[]{:T(128)}, bf16[512,512]{1,0:T(8,128)(2,1)S(1)}, bf16[4,512,512]{2,1,0:T(8,128)(2,1)}, s32[]{:T(128)}) %tuple.67), condition=%wide.region_2.3_spmd, body=%wide.region_1.2_spmd.sunk | while | flops 2 | bytes 4194409 | solution.py:128
  704.0 29.8 fusion.61
  813.3 398.4 %collective-permute-done.2 = bf16[640,7680]{1,0:T(8,128)(2,1)} collective-permute-done((bf16[640,7680]{1,0:T(8,128)(2,1)}, bf16[640,7680]{1,0:T(8,128)(2,1)}, u32[]{:S(2)}, u32[]{:S(2)}) %collective-permute-start.2) | collective-permute-done | bytes 9830432 | tf_op jit(solution)/shard_map/ppermute | solution.py:24
  1211.8 318.0 %collective-permute-done.3 = bf16[640,7680]{1,0:T(8,128)(2,1)} collective-permute-done((bf16[640,7680]{1,0:T(8,128)(2,1)}, bf16[640,7680]{1,0:T(8,128)(2,1)}, u32[]{:S(2)}, u32[]{:S(2)}) %collective-permute-start.3) | collective-permute-done | bytes 9830432 | tf_op jit(solution)/shard_map/ppermute | solution.py:24
  1529.8 31.6 pad_maximum_fusion
  1689.2 29.2 fusion.65
  1718.4 40.0 %multiply_convert_fusion.1 = (bf16[512,7680]{1,0:T(8,128)(2,1)}, bf16[512,7680]{1,0:T(8,128)(2,1)}, bf16[512,7680]{1,0:T(8,128)(2,1)}) fusion(f32[512,7680]{1,0:T(8,128)} %fusion.64, f32[512,7680]{1,0:T(8,128)} %fusion.65, bf16[512,2560]{1,0:T(8,128)(2,1)S(1)} %copy-done.4, bf16[2560,7680]{0,1:T(8,128)(2,1)} %all-gather.36.cloned.1.call-done), kind=kOutput, calls=%fused_computation.33 | convolution fusion | flops 20234895360 | bytes 96993280 | tf_op jit(solution)/shard_map/dot_general | solution.py:186
  1814.7 215.7 %all-to-all-done.5 = bf16[512,8,960]{0,2,1:T(8,128)(2,1)} async-done(((bf16[512,8,960]{0,2,1:T(8,128)(2,1)}), bf16[512,8,960]{0,2,1:T(8,128)(2,1)}, u32[]{:S(2)}, u32[]{:S(2)}) %all-to-all-start.5) | async-done | bytes 7864352 | tf_op jit(solution)/shard_map/all_to_all | solution.py:199
  2030.4 46.3 %all-to-all-start.4 = ((bf16[512,8,960]{0,2,1:T(8,128)(2,1)}), bf16[512,8,960]{0,2,1:T(8,128)(2,1)}, u32[]{:S(2)}, u32[]{:S(2)}) async-start(bf16[512,8,960]{0,2,1:T(8,128)(2,1)} %bitcast.117), calls=%async_computation.4 | async-start | bytes 15728640 | tf_op jit(solution)/shard_map/all_to_all | solution.py:198
  2076.8 29.2 multiply_reduce_fusion.1
  2124.9 189.7 %all-to-all-done.4 = bf16[512,8,960]{0,2,1:T(8,128)(2,1)} async-done(((bf16[512,8,960]{0,2,1:T(8,128)(2,1)}), bf16[512,8,960]{0,2,1:T(8,128)(2,1)}, u32[]{:S(2)}, u32[]{:S(2)}) %all-to-all-start.4) | async-done | bytes 7864352 | tf_op jit(solution)/shard_map/all_to_all | solution.py:198
  2314.7 31.8 all-to-all-start.3
  2380.2 180.2 %all-to-all-done.3 = bf16[512,8,960]{0,2,1:T(8,128)(2,1)} async-done(((bf16[512,8,960]{0,2,1:T(8,128)(2,1)}), bf16[512,8,960]{0,2,1:T(8,128)(2,1)}, u32[]{:S(2)}, u32[]{:S(2)}) %all-to-all-start.3) | async-done | bytes 7864352 | tf_op jit(solution)/shard_map/all_to_all | solution.py:197
  2560.4 67.3 %all-to-all-start.2 = ((bf16[512,8,320]{0,2,1:T(8,128)(2,1)}), bf16[512,8,320]{0,2,1:T(8,128)(2,1)}, u32[]{:S(2)}, u32[]{:S(2)}) async-start(bf16[512,8,320]{0,2,1:T(8,128)(2,1)} %bitcast.126), calls=%async_computation.2 | async-start | bytes 5242880 | tf_op jit(solution)/shard_map/all_to_all | solution.py:266
  2684.3 192.8 %all-gather.46.cloned.1.call-done = bf16[4096,2560]{1,0:T(8,128)(2,1)} async-done(((bf16[512,2560]{1,0:T(8,128)(2,1)}), bf16[4096,2560]{1,0:T(8,128)(2,1)}) %all-gather.46.cloned.1.call-update) | async-done | bytes 20971536 | tf_op jit(solution)/shard_map/all_gather | solution.py:194
  2965.2 34.0 multiply_reduce_fusion
  2999.2 41.7 %multiply_convert_fusion = bf16[5120,2560]{0,1:T(8,128)(2,1)} fusion(f32[5120,2560]{0,1:T(8,128)} %get-tuple-element.123, f32[5120,2560]{0,1:T(8,128)} %get-tuple-element.118, f32[5120]{0:T(1024)S(1)} %get-tuple-element.122, f32[5120]{0:T(1024)S(1)} %log_add_fusion), kind=kLoop, calls=%fused_computation.10 | loop fusion | flops 52428800 | bytes 131112960 | tf_op jit(solution)/shard_map/convert_element_type | solution.py:226
  3070.2 197.3 %while.24 = (s32[]{:T(128)}, f32[512,512]{1,0:T(8,128)S(1)}, f32[4,512,512]{2,1,0:T(8,128)}, s32[]{:T(128)}, s32[]{:T(128)}) while((s32[]{:T(128)}, f32[512,512]{1,0:T(8,128)S(1)}, f32[4,512,512]{2,1,0:T(8,128)}, s32[]{:T(128)}, s32[]{:T(128)}) %tuple.107), condition=%wide.region_9.10_spmd.clone, body=%wide.region_8.9_spmd.clone.sunk | while | flops 1048579 | bytes 6291571 | solution.py:240
  3073.0 72.4 %collective-permute-done.1 = bf16[512,512]{1,0:T(8,128)(2,1)S(1)} collective-permute-done((bf16[512,512]{1,0:T(8,128)(2,1)S(1)}, bf16[512,512]{1,0:T(8,128)(2,1)S(1)}, u32[]{:S(2)}, u32[]{:S(2)}) %collective-permute-start.1) | collective-permute-done | bytes 524320 | tf_op jit(solution)/shard_map/while/body/eval_jaxpr/ppermute | solution.py:36
  3148.4 40.5 %collective-permute-done.1 = bf16[512,512]{1,0:T(8,128)(2,1)S(1)} collective-permute-done((bf16[512,512]{1,0:T(8,128)(2,1)S(1)}, bf16[512,512]{1,0:T(8,128)(2,1)S(1)}, u32[]{:S(2)}, u32[]{:S(2)}) %collective-permute-start.1) | collective-permute-done | bytes 524320 | tf_op jit(solution)/shard_map/while/body/eval_jaxpr/ppermute | solution.py:36
  3191.8 34.0 collective-permute-done.1
  3228.8 38.5 collective-permute-done.1
  3366.3 34.3 all-to-all-done
  3413.5 358.9 %all-gather.42.cloned.1.call-done = bf16[4096,2560]{1,0:T(8,128)(2,1)} async-done(((bf16[512,2560]{1,0:T(8,128)(2,1)}), bf16[4096,2560]{1,0:T(8,128)(2,1)}) %all-gather.42.cloned.1.call-update) | async-done | bytes 20971536 | tf_op jit(solution)/shard_map/all_gather | solution.py:261
  3802.3 41.8 %all-reduce.10 = (f32[2560]{0:T(1024)S(1)}, f32[2560]{0:T(1024)S(1)}) all-reduce(f32[2560]{0:T(1024)S(1)} %get-tuple-element.72, f32[2560]{0:T(1024)S(1)} %copy-done.51), channel_id=3, replica_groups=mesh['dp'=4,'seq'=8] {'dp','seq'}, use_global_device_ids=true, to_apply=%region_13.14.clone | all-reduce | flops 5120 | bytes 40960
  3906.0 33.1 reduce-scatter.7.cloned.1.call-done
  (332 shorter events, 846.4 us)
Async XLA Ops:
  7.2 70.7 %all-gather.18.cloned.1.call-start = ((), (), s32[]{:S(2)}) async-start(), calls=%async_computation.8 | async-start | bytes 3686400 | tf_op jit(solution)/shard_map/all_gather | solution.py:89
  7.9 132.7 %all-gather.24.cloned.1.call-start = ((), (), s32[]{:S(2)}) async-start(), calls=%async_computation.11 | async-start | bytes 3686400 | tf_op jit(solution)/shard_map/all_gather | solution.py:91
  8.7 275.1 %all-gather.30.cloned.1.call-start = ((), (), s32[]{:S(2)}) async-start(), calls=%async_computation.14 | async-start | bytes 11059200 | tf_op jit(solution)/shard_map/all_gather | solution.py:93
  9.4 416.8 %all-gather.34.cloned.1.call-start = ((), (), s32[]{:S(2)}) async-start(), calls=%async_computation.16 | async-start | bytes 11059200 | tf_op jit(solution)/shard_map/all_gather | solution.py:94
  10.0 558.7 %all-gather.28.cloned.1.call-start = ((), (), s32[]{:S(2)}) async-start(), calls=%async_computation.13 | async-start | bytes 11059200 | tf_op jit(solution)/shard_map/all_gather | solution.py:92
  10.6 593.0 %all-gather.22.cloned.1.call-start = ((), (), s32[]{:S(2)}) async-start(), calls=%async_computation.10 | async-start | bytes 3276800 | tf_op jit(solution)/shard_map/all_gather | solution.py:100
  47.6 632.8 %all-gather.20.cloned.1.call-start = ((), (), s32[]{:S(2)}) async-start(), calls=%async_computation.9 | async-start | bytes 16384000 | tf_op jit(solution)/shard_map/all_gather | solution.py:99
  77.9 699.1 %all-gather.26.cloned.1.call-start = ((), (), s32[]{:S(2)}) async-start(), calls=%async_computation.12 | async-start | bytes 16384000 | tf_op jit(solution)/shard_map/all_gather | solution.py:101
  140.6 1548.6 %all-gather.32.cloned.1.call-start = ((), (), s32[]{:S(2)}) async-start(), calls=%async_computation.15 | async-start | bytes 49152000 | tf_op jit(solution)/shard_map/all_gather | solution.py:103
  283.7 1434.7 %all-gather.36.cloned.1.call-start = ((), (), s32[]{:S(2)}) async-start(), calls=%async_computation.17 | async-start | bytes 49152000 | tf_op jit(solution)/shard_map/all_gather | solution.py:104
  426.3 1359.7 %all-gather.38.cloned.1.call-start = ((), (), s32[]{:S(2)}) async-start(), calls=%async_computation.18 | async-start | bytes 49152000 | tf_op jit(solution)/shard_map/all_gather | solution.py:181
  568.7 2066.7 %all-gather.44.cloned.1.call-start = ((), (), s32[]{:S(2)}) async-start(), calls=%async_computation.21 | async-start | bytes 23592960 | tf_op jit(solution)/shard_map/all_gather | solution.py:193
  625.4 15.3 collective-permute-start
  641.6 14.6 collective-permute-start
  796.9 2080.3 %all-gather.46.cloned.1.call-start = ((), (), s32[]{:S(2)}) async-start(), calls=%async_computation.22 | async-start | bytes 23592960 | tf_op jit(solution)/shard_map/all_gather | solution.py:194
  797.6 2559.8 %all-gather.40.cloned.1.call-start = ((), (), s32[]{:S(2)}) async-start(), calls=%async_computation.19 | async-start | bytes 23592960 | tf_op jit(solution)/shard_map/all_gather | solution.py:260
  811.5 400.2 %collective-permute-start.2 = (bf16[640,7680]{1,0:T(8,128)(2,1)}, bf16[640,7680]{1,0:T(8,128)(2,1)}, u32[]{:S(2)}, u32[]{:S(2)}) collective-permute-start(bf16[640,7680]{1,0:T(8,128)(2,1)} %copy.91), channel_id=1, source_target_pairs={{0,8},{8,16},{16,24},{24,0},{1,9},{9,17},{17,25},{25,1},{2,10},{10... | collective-permute-start | bytes 29491208 | tf_op jit(solution)/shard_map/ppermute | solution.py:24
  811.8 399.9 %collective-permute-start.4 = (bf16[640,7680]{1,0:T(8,128)(2,1)}, bf16[640,7680]{1,0:T(8,128)(2,1)}, u32[]{:S(2)}, u32[]{:S(2)}) collective-permute-start(bf16[640,7680]{1,0:T(8,128)(2,1)} %copy.91), channel_id=1, source_target_pairs={{8,0},{16,8},{24,16},{0,24},{9,1},{17,9},{25,17},{1,25},{10,2},{18... | collective-permute-start | bytes 29491208 | tf_op jit(solution)/shard_map/ppermute | solution.py:26
  1211.7 318.1 %collective-permute-start.3 = (bf16[640,7680]{1,0:T(8,128)(2,1)}, bf16[640,7680]{1,0:T(8,128)(2,1)}, u32[]{:S(2)}, u32[]{:S(2)}) collective-permute-start(bf16[640,7680]{1,0:T(8,128)(2,1)} %collective-permute-done.2), channel_id=1, source_target_pairs={{0,8},{8,16},{16,24},{24,0},{1,9},{9,17},{17,25},{25,1},{2,10},{10... | collective-permute-start | bytes 29491208 | tf_op jit(solution)/shard_map/ppermute | solution.py:24
  1769.0 261.4 %all-to-all-start.5 = ((bf16[512,8,960]{0,2,1:T(8,128)(2,1)}), bf16[512,8,960]{0,2,1:T(8,128)(2,1)}, u32[]{:S(2)}, u32[]{:S(2)}) async-start(bf16[512,8,960]{0,2,1:T(8,128)(2,1)} %bitcast.119), calls=%async_computation.5 | async-start | bytes 15728640 | tf_op jit(solution)/shard_map/all_to_all | solution.py:199
  2030.4 284.3 %all-to-all-start.4 = ((bf16[512,8,960]{0,2,1:T(8,128)(2,1)}), bf16[512,8,960]{0,2,1:T(8,128)(2,1)}, u32[]{:S(2)}, u32[]{:S(2)}) async-start(bf16[512,8,960]{0,2,1:T(8,128)(2,1)} %bitcast.117), calls=%async_computation.4 | async-start | bytes 15728640 | tf_op jit(solution)/shard_map/all_to_all | solution.py:198
  2076.7 1695.7 %all-gather.42.cloned.1.call-start = ((), (), s32[]{:S(2)}) async-start(), calls=%async_computation.20 | async-start | bytes 23592960 | tf_op jit(solution)/shard_map/all_gather | solution.py:261
  2314.7 245.8 %all-to-all-start.3 = ((bf16[512,8,960]{0,2,1:T(8,128)(2,1)}), bf16[512,8,960]{0,2,1:T(8,128)(2,1)}, u32[]{:S(2)}, u32[]{:S(2)}) async-start(bf16[512,8,960]{0,2,1:T(8,128)(2,1)} %bitcast.118), calls=%async_computation.3 | async-start | bytes 15728640 | tf_op jit(solution)/shard_map/all_to_all | solution.py:197
  2560.4 726.9 %all-to-all-start.2 = ((bf16[512,8,320]{0,2,1:T(8,128)(2,1)}), bf16[512,8,320]{0,2,1:T(8,128)(2,1)}, u32[]{:S(2)}, u32[]{:S(2)}) async-start(bf16[512,8,320]{0,2,1:T(8,128)(2,1)} %bitcast.126), calls=%async_computation.2 | async-start | bytes 5242880 | tf_op jit(solution)/shard_map/all_to_all | solution.py:266
  2627.8 1266.1 %reduce-scatter.9.cloned.1.call-start = ((), (), s32[]{:S(2)}) async-start(), calls=%async_computation.24 | async-start | bytes 18841600
  3071.7 73.7 %collective-permute-start.1 = (bf16[512,512]{1,0:T(8,128)(2,1)S(1)}, bf16[512,512]{1,0:T(8,128)(2,1)S(1)}, u32[]{:S(2)}, u32[]{:S(2)}) collective-permute-start(bf16[512,512]{1,0:T(8,128)(2,1)S(1)} %fusion.108), channel_id=1, source_target_pairs={{1,0},{2,1},{3,2},{4,3},{5,4},{6,5},{7,6},{9,8},{10,9},{11,10},{12... | collective-permute-start | bytes 1572872 | tf_op jit(solution)/shard_map/while/body/eval_jaxpr/ppermute | solution.py:36
  3147.1 41.8 %collective-permute-start.1 = (bf16[512,512]{1,0:T(8,128)(2,1)S(1)}, bf16[512,512]{1,0:T(8,128)(2,1)S(1)}, u32[]{:S(2)}, u32[]{:S(2)}) collective-permute-start(bf16[512,512]{1,0:T(8,128)(2,1)S(1)} %fusion.108), channel_id=1, source_target_pairs={{1,0},{2,1},{3,2},{4,3},{5,4},{6,5},{7,6},{9,8},{10,9},{11,10},{12... | collective-permute-start | bytes 1572872 | tf_op jit(solution)/shard_map/while/body/eval_jaxpr/ppermute | solution.py:36
  3190.5 35.3 collective-permute-start.1
  3227.5 39.8 %collective-permute-start.1 = (bf16[512,512]{1,0:T(8,128)(2,1)S(1)}, bf16[512,512]{1,0:T(8,128)(2,1)S(1)}, u32[]{:S(2)}, u32[]{:S(2)}) collective-permute-start(bf16[512,512]{1,0:T(8,128)(2,1)S(1)} %fusion.108), channel_id=1, source_target_pairs={{1,0},{2,1},{3,2},{4,3},{5,4},{6,5},{7,6},{9,8},{10,9},{11,10},{12... | collective-permute-start | bytes 1572872 | tf_op jit(solution)/shard_map/while/body/eval_jaxpr/ppermute | solution.py:36
  3287.3 21.7 all-to-all-start.1
  3309.0 91.6 %all-to-all-start = ((bf16[512,8,320]{0,2,1:T(8,128)(2,1)}), bf16[512,8,320]{0,2,1:T(8,128)(2,1)S(1)}, u32[]{:S(2)}, u32[]{:S(2)}) async-start(bf16[512,8,320]{0,2,1:T(8,128)(2,1)} %bitcast.129), calls=%async_computation | async-start | bytes 5242880 | tf_op jit(solution)/shard_map/all_to_all | solution.py:264
  3328.1 610.9 %reduce-scatter.7.cloned.1.call-start = ((), (), s32[]{:S(2)}) async-start(), calls=%async_computation.23 | async-start | bytes 4915200
  (66 other events, 2127.8 us)
Sparse Core Ops, SparseCore 0:
  10.2 67.6 all-gather.17
  80.1 60.4 all-gather.23
  142.8 140.8 all-gather.29
  285.8 140.3 all-gather.33
  428.2 140.3 all-gather.27
  570.1 23.6 all-gather.21
  595.4 84.9 all-gather.19
  682.0 84.9 all-gather.25
  768.5 421.8 all-gather.31
  1191.9 340.1 all-gather.35
  1533.7 235.5 all-gather.37
  1770.7 621.3 all-gather.43
  2393.7 483.4 all-gather.45
  2879.1 478.2 all-gather.39
  3358.8 413.5 all-gather.41
  3774.9 118.9 reduce-scatter.8
  3896.3 42.7 reduce-scatter.6
